TPU v7x, 16 devices: a 4x2x1 block of a 4x4x8 slice. The times are simulated.
16 devices in a mesh: dp: 2 (over y, z), tp: 8 (over x, core).
Axes of the slice: x: 4, y: 2, z: 1, core: 2. Of those that a mesh axis runs over, the one named last changes fastest.
The devices are a block of a 4x4x8 slice.
Arguments:
- x: bfloat16 [8192, 2048], P(('dp', 'tp')), parts along dimension 0
- dy: bfloat16 [8192, 2048], P(('dp', 'tp')), parts along dimension 0
- gate: bfloat16 [8192, 8192], P('dp', 'tp'), parts along dimension 0
- up: bfloat16 [8192, 8192], P('dp', 'tp'), parts along dimension 0
- w_gate: bfloat16 [2048, 8192], P(None, 'tp')
- w_up: bfloat16 [2048, 8192], P(None, 'tp')
- w_down: bfloat16 [8192, 2048], P('tp')
Outputs:
- output 1: bfloat16 [8192, 2048], P(('dp', 'tp')), parts along dimension 0
- output 2: bfloat16 [4096, 8192], P('dp', 'tp'), parts along dimension 0
- output 3: bfloat16 [4096, 8192], P('dp', 'tp'), parts along dimension 0
- output 4: bfloat16 [16384, 2048], P(('dp', 'tp')), parts along dimension 0
There are 2 independent parts. A program takes and returns all parts, laid end to end along the dimension named above; an argument that names none is the same for every part.
All inputs are finite; a program needn't handle non-finite values.
Results may differ from a plain program's by a relative error of at most 0.012.
Values are sent between devices in bfloat16 or wider.
A program may use at most 768 MiB of HBM per device.

v0:
```python
import jax
import jax.numpy as jnp


def act(gate, up):
    return jax.nn.silu(gate) * up


def solution(mesh):
    def step(x, dy, gate, up, w_gate, w_up, w_down):
        hidden, back = jax.vjp(act, gate.astype(jnp.float32), up.astype(jnp.float32))
        d_hidden = jnp.dot(dy, w_down.T, preferred_element_type=jnp.float32)
        d_gate, d_up = (g.astype(jnp.bfloat16) for g in back(d_hidden))
        dx = jnp.dot(d_gate, w_gate.T) + jnp.dot(d_up, w_up.T)
        groups = mesh.shape["dp"]

        def by_group(a, b):
            a, b = (t.reshape(groups, -1, t.shape[-1]) for t in (a, b))
            product = jnp.einsum("gta,gtb->gab", a, b, preferred_element_type=jnp.float32)
            return product.astype(jnp.bfloat16).reshape(-1, b.shape[-1])

        return dx, by_group(x, d_gate), by_group(x, d_up), by_group(hidden.astype(jnp.bfloat16), dy)

    return step
```

profile of v0, /device:TPU:112, one launch (start us, length us, event | category | flops | bytes accessed | tf_op | source)
XLA Modules:
  0.0 274.6 jit_solution(1885693060200692130)
XLA Ops:
  7.2 0.1 all-gather.11.cloned.1.call-start
  7.2 0.7 all-gather.11.cloned.1.call-update
  8.0 0.1 all-gather.13.cloned.1.call-start
  8.0 0.7 all-gather.13.cloned.1.call-update
  8.8 0.1 reduce-scatter.4.cloned.1.call-start
  8.9 84.7 %all-gather.11.cloned.1.call-done = bf16[4096,2048]{1,0:T(8,128)(2,1)} async-done(((bf16[512,2048]{1,0:T(8,128)(2,1)}), bf16[4096,2048]{1,0:T(8,128)(2,1)}) %all-gather.11.cloned.1.call-update) | async-done | bytes 16777232 | tf_op args[1]
  93.6 32.7 %multiply_convert_fusion = (bf16[4096,1024]{1,0:T(8,128)(2,1)}, bf16[4096,1024]{1,0:T(8,128)(2,1)}) fusion(bf16[4096,1024]{1,0:T(8,128)(2,1)} %param.3, bf16[4096,1024]{1,0:T(8,128)(2,1)} %param.2, bf16[4096,2048]{1,0:T(8,128)(2,1)} %all-gather.11.cloned.1.call-done, bf16[1024,2048]{1,0:T(8,128)(2,1)} %param.1), kind=kOutput, calls=%fused_computation.13 | convolution fusion | flops 17246978048 | bytes 54525952 | tf_op jit(solution)/dot_general | solution.py:12
  126.3 23.5 %fusion.13 = bf16[4096,2048]{1,0:T(8,128)(2,1)} fusion(bf16[4096,1024]{1,0:T(8,128)(2,1)} %get-tuple-element.5, bf16[2048,1024]{1,0:T(8,128)(2,1)} %param.4), kind=kOutput, calls=%fused_computation.20 | convolution fusion | flops 17179869184 | bytes 29360128 | tf_op jit(solution)/dot_general | solution.py:14
  149.8 25.2 %convolution_add_fusion = bf16[4096,2048]{1,0:T(8,128)(2,1)} fusion(bf16[4096,2048]{1,0:T(8,128)(2,1)} %fusion.13, bf16[4096,1024]{1,0:T(8,128)(2,1)} %get-tuple-element.4, bf16[2048,1024]{1,0:T(8,128)(2,1)} %param.5), kind=kOutput, calls=%fused_computation.14 | convolution fusion | flops 17188257792 | bytes 46137344 | tf_op jit(solution)/dot_general | solution.py:14
  175.0 0.1 reduce-scatter.4.cloned.1.call-update
  175.1 1.8 all-gather.13.cloned.1.call-done
  176.8 23.8 %convert_bitcast_fusion.1 = bf16[2048,1024]{0,1:T(8,128)(2,1)} fusion(bf16[4096,1024]{1,0:T(8,128)(2,1)} %get-tuple-element.5, bf16[4096,2048]{1,0:T(8,128)(2,1)} %all-gather.13.cloned.1.call-done), kind=kOutput, calls=%fused_computation.17 | convolution fusion | flops 17181966336 | bytes 29360128 | tf_op jit(solution)/gta,gtb->gab/dot_general | solution.py:19
  200.6 6.4 %copy = bf16[2048,1024]{1,0:T(8,128)(2,1)} copy(bf16[2048,1024]{0,1:T(8,128)(2,1)} %convert_bitcast_fusion.1) | data formatting | bytes 8388608
  207.0 23.8 %convert_bitcast_fusion = bf16[2048,1024]{0,1:T(8,128)(2,1)} fusion(bf16[4096,1024]{1,0:T(8,128)(2,1)} %get-tuple-element.4, bf16[4096,2048]{1,0:T(8,128)(2,1)} %all-gather.13.cloned.1.call-done), kind=kOutput, calls=%fused_computation.16 | convolution fusion | flops 17181966336 | bytes 29360128 | tf_op jit(solution)/gta,gtb->gab/dot_general | solution.py:19
  230.8 6.4 %copy.1 = bf16[2048,1024]{1,0:T(8,128)(2,1)} copy(bf16[2048,1024]{0,1:T(8,128)(2,1)} %convert_bitcast_fusion) | data formatting | bytes 8388608
  237.2 27.1 %fusion.9 = bf16[1024,2048]{1,0:T(8,128)(2,1)} fusion(bf16[4096,2048]{1,0:T(8,128)(2,1)} %all-gather.11.cloned.1.call-done, bf16[4096,1024]{1,0:T(8,128)(2,1)} %param.2, bf16[4096,1024]{1,0:T(8,128)(2,1)} %param.3), kind=kOutput, calls=%fused_computation.18 | convolution fusion | flops 17215520768 | bytes 37748736 | tf_op jit(solution)/gta,gtb->gab/dot_general | solution.py:19
  264.2 3.8 %reduce-scatter.4.cloned.1.call-done = bf16[512,2048]{1,0:T(8,128)(2,1)} async-done(((bf16[4096,2048]{1,0:T(8,128)(2,1)}), bf16[512,2048]{1,0:T(8,128)(2,1)}) %reduce-scatter.4.cloned.1.call-update) | async-done | bytes 2097168
Async XLA Ops:
  7.2 86.4 %all-gather.11.cloned.1.call-start = ((), (), s32[]{:S(2)}) async-start(), calls=%async_computation.1 | async-start | bytes 18874368 | tf_op args[1]
  8.0 168.9 %all-gather.13.cloned.1.call-start = ((), (), s32[]{:S(2)}) async-start(), calls=%async_computation.2 | async-start | bytes 18874368 | tf_op jit(solution)/reshape | solution.py:18
  8.8 259.3 %reduce-scatter.4.cloned.1.call-start = ((), (), s32[]{:S(2)}) async-start(), calls=%async_computation.3 | async-start | bytes 18874368
Sparse Core Ops, SparseCore 0:
  9.6 83.9 all-gather.10
  95.2 81.6 all-gather.12
  179.8 88.2 reduce-scatter.3
where the time goes:
time: 275 us
  matrix products  156 us (57%)
  waiting for transfers between devices  91.9 us (33%)
  between operations  13.8 us (5%)
  local copies, waits for them, and re-layouts  12.8 us (5%)
    unnamed x5, waiting for transfers between devices  90.1 us
    dot_general x3, matrix products, by_group(): jnp.einsum('gta,gtb->gab', a, b, preferred_element_type=jnp.float32)  74.6 us
    dot_general x2, matrix products, step(): dx = jnp.dot(d_gate, w_gate.T) + jnp.dot(d_up, w_up.T)  48.7 us
    dot_general x1, matrix products, step(): d_hidden = jnp.dot(dy, w_down.T, preferred_element_type=jnp.float32)  32.7 us
    unnamed x2, local copies, waits for them, and re-layouts  12.8 us
  transfers between devices with their start and end apart: 3, of which 3 were waited for; matrix products, arithmetic and copies ran while one was open for 61% of the time, Pallas kernels for 0%

commit v1 on v0

v1 whole, which is shorter than its diff:
```python
import functools

import jax
import jax.numpy as jnp
from jax import lax
from jax.experimental import pallas as pl
from jax.experimental.pallas import tpu as pltpu
from jax.sharding import PartitionSpec as P

MESH = pl.DeviceIdType.MESH
NT = (((1,), (1,)), ((), ()))
TN = (((0,), (0,)), ((), ()))
F32, BF16 = jnp.float32, jnp.bfloat16
OWN, RIGHT, LEFT, OPP = range(4)
CHIP_STEP = (0, 1, 3, 2)

POS_A, POS_B, NEG_B, NEG_A, FWD_POS, FWD_NEG, SIB = range(7)
X0 = 10
SUM_SIB = 20
U2_POS, U2_NEG, U1_POS, U1_NEG, U3_POS, U3_NEG = range(24, 30)
N_COPIES = 30


def dot(a, b, dims):
    return lax.dot_general(a, b, dims, preferred_element_type=F32)


def kernel(n, x, dy, gate, up, wg_in, wu_in, wd_in,
           dx, dwg, dwu, dwd, dyf, xf, dgs, dus, sibr, sumr,
           wd, wg, wu, accd, accg, accu, act, gb, ub, dgb, dub, hb, sibst, sumst, last,
           send, recv, lsem, ssem, wsem):
    rows, d = x.shape
    f = gate.shape[1]
    half = rows // 2
    me = lax.axis_index("tp")
    core = lax.rem(me, 2)
    chip = lax.div(me, 2)
    chips = n // 2
    right, left = lax.rem(me + 2, n), lax.rem(me + n - 2, n)
    sib = me + 1 - 2 * core

    def at(ref, start, size):
        if not isinstance(start, int):
            start = pl.multiple_of(start, size)
        return ref.at[pl.ds(start, size)]

    def slot(q, m, h=None):
        return (q * 2 + m) * rows + (0 if h is None else h * half)

    def token(q, m):
        ahead = CHIP_STEP[q] if isinstance(q, int) else q + lax.div(q, 2) * (5 - 2 * q)
        c = lax.rem(chip + ahead, chips)
        k = core + m - 2 * core * m
        return (c * 2 + k) * rows

    def remote(i, src, dst, to):
        return pltpu.make_async_remote_copy(
            src_ref=src, dst_ref=dst, send_sem=send.at[i], recv_sem=recv.at[i],
            device_id={"tp": to}, device_id_type=MESH)

    def gather_copies(base, own, full):
        blk = lambda q, m: at(full, slot(q, m), rows)
        hlf = lambda q, h: at(full, slot(q, 0, h), half)
        mine = lambda h: at(own, h * half, half)
        copies = {
            POS_A: (mine(0), hlf(LEFT, 0), right),
            POS_B: (mine(1), hlf(LEFT, 1), right),
            NEG_B: (mine(1), hlf(RIGHT, 1), left),
            NEG_A: (mine(0), hlf(RIGHT, 0), left),
            FWD_POS: (hlf(LEFT, 0), hlf(OPP, 0), right),
            FWD_NEG: (hlf(RIGHT, 1), hlf(OPP, 1), left),
            SIB + OWN: (own, blk(OWN, 1), sib),
        }
        for q in (RIGHT, LEFT, OPP):
            copies[SIB + q] = (blk(q, 0), blk(q, 1), sib)
        return {i: remote(base + i, *c) for i, c in copies.items()}

    cdy = gather_copies(0, dy, dyf)
    cx = gather_copies(X0, x, xf)
    csib = [remote(SUM_SIB + q, sibst.at[q % 2], at(sibr, q * rows, rows), sib) for q in range(4)]
    su = lambda i, s, to, dst: remote(i, sumst.at[s], dst, to)
    c2 = [su(U2_POS, 0, right, at(sumr, 0, half)), su(U2_NEG, 1, left, at(sumr, half, half))]
    c1 = [su(U1_POS, 2, right, at(sumr, 2 * half, half)), su(U1_NEG, 3, left, at(sumr, 3 * half, half))]
    c3 = [su(U3_POS, 0, right, last.at[0]), su(U3_NEG, 1, left, last.at[1])]

    barrier = pltpu.get_barrier_semaphore()
    for other in (left, right, sib):
        pl.semaphore_signal(barrier, inc=1, device_id={"tp": other}, device_id_type=MESH)
    pl.semaphore_wait(barrier, 3)

    for i in (POS_A, NEG_B, POS_B, NEG_A, SIB + OWN):
        cdy[i].start()
    cx[SIB + OWN].start()
    weights = [pltpu.make_async_copy(s, t, wsem.at[i]) for i, (s, t) in enumerate(((wd_in, wd), (wg_in, wg), (wu_in, wu)))]
    weights[0].start()

    def load(src, dst, sem):
        return pltpu.make_async_copy(src, dst, sem)

    def start_block(own, full, first, second, q, m, r, b):
        big = act.at[b]
        if own is None:
            load(at(full, slot(q, m), rows), big, lsem.at[b, 0]).start()
        else:
            @pl.when(m == 0)
            def _():
                load(own, big, lsem.at[b, 0]).start()

            @pl.when(m != 0)
            def _():
                load(at(full, slot(q, m), rows), big, lsem.at[b, 0]).start()
        load(at(first, r, rows), gb.at[b], lsem.at[b, 1]).start()
        load(at(second, r, rows), ub.at[b], lsem.at[b, 2]).start()

    def wait_block(b):
        load(dy, act.at[b], lsem.at[b, 0]).wait()
        load(at(gate, 0, rows), gb.at[b], lsem.at[b, 1]).wait()
        load(at(gate, 0, rows), ub.at[b], lsem.at[b, 2]).wait()

    def blocks(count, place, ready, begin, compute):
        ready(0)
        begin(*place(0), 0)

        def body(i, _):
            b = lax.rem(i, 2)
            wait_block(b)

            @pl.when(i + 1 < count)
            def _():
                ready(i + 1)
                begin(*place(i + 1), 1 - b)

            compute(*place(i), b)
            return 0

        lax.fori_loop(0, count, body, 0)

    tile_f = 512 if f % 512 == 0 else f
    tile_d = 512 if d % 512 == 0 else d

    def begin_dy(own):
        return lambda q, m, b: start_block(own, dyf, gate, up, q, m, token(q, m), b)

    def from_dy(q, m, b):
        def columns(j, _):
            c = pl.ds(pl.multiple_of(j * tile_f, tile_f), tile_f)
            d_hidden = dot(act[b], wd[c, :], NT)
            g, u = gb[b, :, c].astype(F32), ub[b, :, c].astype(F32)
            s = lax.logistic(g)
            silu = g * s
            hb[:, c] = (silu * u).astype(BF16)
            dub[:, c] = (d_hidden * silu).astype(BF16)
            t = d_hidden * u
            dgb[:, c] = (t * s + t * g * (s * (1.0 - s))).astype(BF16)
            return 0

        lax.fori_loop(0, f // tile_f, columns, 0)
        r = slot(q, m)
        saves = [load(dgb, at(dgs, r, rows), ssem.at[0]), load(dub, at(dus, r, rows), ssem.at[1])]
        for s in saves:
            s.start()

        def hidden_columns(j, _):
            c = pl.ds(pl.multiple_of(j * tile_f, tile_f), tile_f)
            for k in range(0, d, d // 2):
                accd[c, k : k + d // 2] += dot(hb[:, c], act[b, :, k : k + d // 2], TN)
            return 0

        lax.fori_loop(0, f // tile_f, hidden_columns, 0)
        for s in saves:
            s.wait()

    def begin_x(own):
        return lambda q, m, b: start_block(own, xf, dgs, dus, q, m, slot(q, m), b)

    def from_x(q, m, b):
        def columns(j, _):
            c = pl.ds(pl.multiple_of(j * tile_d, tile_d), tile_d)
            xt = act[b, :, c]
            accg[c, :] += dot(xt, gb[b], TN)
            accu[c, :] += dot(xt, ub[b], TN)
            return 0

        lax.fori_loop(0, d // tile_d, columns, 0)

    def dx_rows(r, count, adds, store):
        loads = [load(at(dgs, r, count), gb.at[0, pl.ds(0, count)], lsem.at[0, 1]), load(at(dus, r, count), ub.at[0, pl.ds(0, count)], lsem.at[0, 2])]
        bufs = [act.at[i, pl.ds(0, count)] for i in range(len(adds))]
        loads += [load(a, t, lsem.at[i, 0]) for i, (a, t) in enumerate(zip(adds, bufs))]
        for o in loads:
            o.start()
        for o in loads:
            o.wait()

        def columns(j, _):
            c = pl.ds(pl.multiple_of(j * tile_d, tile_d), tile_d)
            t = dot(gb[0, :count], wg[c, :], NT) + dot(ub[0, :count], wu[c, :], NT)
            for o in bufs:
                t += o[:, c].astype(F32)
            store(c, t)
            return 0

        lax.fori_loop(0, d // tile_d, columns, 0)

    def dx_for_sibling(q):
        if q >= 2:
            csib[q - 2].wait_send()

        def store(c, t):
            sibst[q % 2, :, c] = t.astype(BF16)

        dx_rows(slot(q, 1), rows, [], store)
        csib[q].start()

    def dx_sum(q, h, s, extra, copy):
        def store(c, t):
            sumst[s, :, c] = t.astype(BF16)

        dx_rows(slot(q, 0, h), half, [at(sibr, q * rows + h * half, half), *extra], store)
        copy.start()

    def zero(ref):
        def body(i, _):
            ref[pl.ds(pl.multiple_of(i * 128, 128), 128), :] = jnp.zeros((128, ref.shape[1]), F32)
            return 0

        lax.fori_loop(0, ref.shape[0] // 128, body, 0)

    nothing = lambda i: None

    def ready_own(copies):
        def ready(i):
            if not isinstance(i, int):
                copies[SIB + OWN].wait_recv()

        return ready

    own_place = lambda i: (0, i)
    weights[1].start()
    weights[2].start()
    for ref in (accd, accg, accu):
        zero(ref)
    weights[0].wait()
    blocks(2, own_place, ready_own(cdy), begin_dy(dy), from_dy)
    weights[1].wait()
    weights[2].wait()
    dx_for_sibling(OWN)

    cdy[POS_A].wait_recv()
    cdy[NEG_B].wait_recv()
    cdy[FWD_POS].start()
    cdy[FWD_NEG].start()
    for i in (POS_A, NEG_B, POS_B, NEG_A):
        cx[i].start()
    blocks(2, own_place, ready_own(cx), begin_x(x), from_x)

    cdy[POS_B].wait_recv()
    cdy[NEG_A].wait_recv()
    cdy[SIB + RIGHT].start()
    cdy[SIB + LEFT].start()

    def ready_near(copies):
        def ready(i):
            if not isinstance(i, int):
                @pl.when(i == 2)
                def _():
                    copies[SIB + RIGHT].wait_recv()
                    copies[SIB + LEFT].wait_recv()

        return ready

    near_place = lambda i: (1 + lax.rem(i, 2), lax.div(i, 2)) if not isinstance(i, int) else (1 + i % 2, i // 2)
    blocks(4, near_place, ready_near(cdy), begin_dy(None), from_dy)
    cdy[FWD_POS].wait_recv()
    cdy[FWD_NEG].wait_recv()
    cdy[SIB + OPP].start()
    dx_for_sibling(RIGHT)
    dx_for_sibling(LEFT)
    csib[RIGHT].wait_recv()
    dx_sum(RIGHT, 1, 0, [], c2[0])
    csib[LEFT].wait_recv()
    dx_sum(LEFT, 0, 1, [], c2[1])

    def ready_far(copies):
        def ready(i):
            if not isinstance(i, int):
                copies[SIB + OPP].wait_recv()

        return ready

    far_place = lambda i: (OPP, i)
    blocks(2, far_place, ready_far(cdy), begin_dy(None), from_dy)
    dx_for_sibling(OPP)
    csib[OPP].wait_recv()
    dx_sum(OPP, 0, 2, [], c1[0])
    dx_sum(OPP, 1, 3, [], c1[1])

    cx[POS_A].wait_recv()
    cx[NEG_B].wait_recv()
    cx[FWD_POS].start()
    cx[FWD_NEG].start()
    cx[POS_B].wait_recv()
    cx[NEG_A].wait_recv()
    cx[SIB + RIGHT].start()
    cx[SIB + LEFT].start()

    csib[LEFT].wait_send()
    csib[OPP].wait_send()
    outs = []
    for i in range(f // rows):
        sibst[i] = accd[i * rows : (i + 1) * rows, :].astype(BF16)
        outs.append(load(sibst.at[i], at(dwd, i * rows, rows), wsem.at[i]))
        outs[-1].start()

    blocks(4, near_place, ready_near(cx), begin_x(None), from_x)

    csib[OWN].wait_recv()
    for h, i in ((1, 0), (0, 1)):
        c2[i].wait_recv()

        def store(c, t, h=h):
            accd[h * half : (h + 1) * half, c] = t

        dx_rows(slot(OWN, 0, h), half, [at(sibr, h * half, half), at(sumr, i * half, half)], store)

    for q, h, i in ((RIGHT, 0, 0), (LEFT, 1, 1)):
        c1[i].wait_recv()
        c2[i].wait_send()
        dx_sum(q, h, i, [at(sumr, (2 + i) * half, half)], c3[i])

    cx[FWD_POS].wait_recv()
    cx[FWD_NEG].wait_recv()
    cx[SIB + OPP].start()
    blocks(2, far_place, ready_far(cx), begin_x(None), from_x)
    for o in outs:
        o.wait()

    outs = []
    for i in range(d // rows):
        b = i % 2
        if i >= 2:
            outs[2 * i - 4].wait()
            outs[2 * i - 3].wait()
        r = slice(i * rows, (i + 1) * rows)
        gb[b] = accg[r, :].astype(BF16)
        outs.append(load(gb.at[b], at(dwg, i * rows, rows), lsem.at[b, 1]))
        outs[-1].start()
        ub[b] = accu[r, :].astype(BF16)
        outs.append(load(ub.at[b], at(dwu, i * rows, rows), lsem.at[b, 2]))
        outs[-1].start()
    for o in outs[-4:]:
        o.wait()

    outs = []
    for i in range(2):
        c3[i].wait_recv()
        r = slice(i * half, (i + 1) * half)
        act[0, r, :] = (accd[r, :] + last[i].astype(F32)).astype(BF16)
        outs.append(load(act.at[0, pl.ds(i * half, half)], at(dx, i * half, half), lsem.at[i, 0]))
        outs[-1].start()
    for o in outs:
        o.wait()
    for c in (*cdy.values(), *cx.values(), *c1, *c3):
        c.wait_send()


def solution(mesh):
    n = mesh.shape["tp"]

    def local(x, dy, gate, up, wg, wu, wd):
        rows, d = x.shape
        tokens, f = gate.shape
        half = rows // 2
        hbm = pl.BlockSpec(memory_space=pltpu.HBM)
        s = lambda *shape: jax.ShapeDtypeStruct(shape, BF16)
        v = lambda *shape: pltpu.VMEM(shape, BF16)
        a = lambda *shape: pltpu.VMEM(shape, F32)
        dma = pltpu.SemaphoreType.DMA
        flops = 12 * tokens * d * f
        outs = pl.pallas_call(
            functools.partial(kernel, n),
            out_shape=(s(rows, d), s(d, f), s(d, f), s(f, d), s(tokens, d), s(tokens, d), s(tokens, f), s(tokens, f), s(4 * rows, d), s(4 * half, d)),
            in_specs=[hbm] * 7,
            out_specs=[hbm] * 10,
            scratch_shapes=[
                v(f, d), v(d, f), v(d, f), a(f, d), a(d, f), a(d, f),
                v(2, rows, d), v(2, rows, f), v(2, rows, f), v(rows, f), v(rows, f), v(rows, f),
                v(2, rows, d), v(4, half, d), v(2, half, d),
                dma((N_COPIES,)), dma((N_COPIES,)), dma((2, 3)), dma((2,)), dma((3,)),
            ],
            compiler_params=pltpu.CompilerParams(collective_id=0, has_side_effects=True, vmem_limit_bytes=67043328),
            cost_estimate=pl.CostEstimate(flops=flops, bytes_accessed=200 * 2**20, transcendentals=tokens * f),
            name="mlp_backward",
        )(x, dy, gate, up, wg, wu, wd)
        return outs[:4]

    rows, columns = P(("dp", "tp"), None), P("dp", "tp")
    return jax.shard_map(
        local,
        mesh=mesh,
        in_specs=(rows, rows, columns, columns, P(None, "tp"), P(None, "tp"), P("tp", None)),
        out_specs=(rows, columns, columns, rows),
        check_vma=False,
    )
```

time: 275 us -> 224 us (0.81)
  Pallas kernels: 0 us -> 210 us
  matrix products: 156 us -> 0 us
  waiting for transfers between devices: 91.9 us -> 0 us
  between operations: 13.8 us -> 0.65 us
    pallas_call x0 -> x1, Pallas kernels: none -> 210 us  [local(): pl.pallas_call(functools.partial(kernel, n), out_shape=(s(rows, d), s(d,...]
    dot_general x6 -> x0, matrix products: 156 us -> none  [the longest x3 74.6 us: by_group(): jnp.einsum('gta,gtb->gab', a, b, preferred_element_type=jnp.float32)]
    unnamed x5 -> x0, waiting for transfers between devices: 90.1 us -> none
    unnamed x2 -> x10, local copies, waits for them, and re-layouts: 12.8 us -> 12.7 us
  transfers between devices with their start and end apart: 3 -> 0, of which waited for: 3 -> 0; matrix products, arithmetic and copies ran while one was open for 61% -> 0% of each run, Pallas kernels for 0% -> 0%
where the time goes in v1:
time: 224 us; the launch traced here: 223 us
  Pallas kernels  210 us (94%)
  local copies, waits for them, and re-layouts  12.7 us (6%)
    pallas_call x1, Pallas kernels, local(): pl.pallas_call(functools.partial(kernel, n), out_shape=(s(rows, d), s(d,...  210 us
    unnamed x10, local copies, waits for them, and re-layouts  12.7 us

profile of v1, /device:TPU:112, one launch (start us, length us, event | category | flops | bytes accessed | tf_op | source)
XLA Modules:
  0.0 223.1 jit_solution(13059347764012544478)
XLA Ops:
  0.6 209.7 %mlp_backward.1 = (bf16[512,2048]{1,0:T(8,128)(2,1)}, bf16[2048,1024]{1,0:T(8,128)(2,1)}, bf16[2048,1024]{1,0:T(8,128)(2,1)}, bf16[1024,2048]{1,0:T(8,128)(2,1)}...) custom-call(bf16[512,2048]{1,0:T(8,128)(2,1)} %x.1, ...), custom_call_target="tpu_custom_call" | custom-call | flops 103079215104 | bytes 209715200 | tf_op jit(solution)/shard_map/mlp_backward/pallas_call | solution.py:380
  210.4 0.0 copy-start.2
  210.4 3.3 %copy.15 = bf16[512,2048]{1,0:T(8,128)(2,1)} copy(bf16[512,2048]{1,0:T(8,128)(2,1)} %get-tuple-element.16) | data formatting | bytes 4194304
  213.7 0.0 copy-done.2
  213.7 0.0 copy-start.1
  213.7 2.1 copy.16
  215.8 1.6 copy-done.1
  217.4 0.0 copy-start
  217.4 2.1 copy.17
  219.5 1.6 copy-done
  221.1 2.0 copy.18
Async XLA Ops:
  210.4 3.3 %copy-start.2 = (bf16[2048,1024]{1,0:T(8,128)(2,1)S(1)}, bf16[2048,1024]{1,0:T(8,128)(2,1)}, u32[]{:S(2)}) copy-start(bf16[2048,1024]{1,0:T(8,128)(2,1)} %get-tuple-element.17) | copy-start | bytes 12582916
  213.7 3.7 %copy-start.1 = (bf16[2048,1024]{1,0:T(8,128)(2,1)S(1)}, bf16[2048,1024]{1,0:T(8,128)(2,1)}, u32[]{:S(2)}) copy-start(bf16[2048,1024]{1,0:T(8,128)(2,1)} %get-tuple-element.18) | copy-start | bytes 12582916
  217.4 3.7 %copy-start = (bf16[1024,2048]{1,0:T(8,128)(2,1)S(1)}, bf16[1024,2048]{1,0:T(8,128)(2,1)}, u32[]{:S(2)}) copy-start(bf16[1024,2048]{1,0:T(8,128)(2,1)} %get-tuple-element.19) | copy-start | bytes 12582916

commit v2 on v1

--- a/solution.py
+++ b/solution.py
@@ -11,6 +11,7 @@
 NT = (((1,), (1,)), ((), ()))
 TN = (((0,), (0,)), ((), ()))
 F32, BF16 = jnp.float32, jnp.bfloat16
+LIMIT = 41 * 2**20
 OWN, RIGHT, LEFT, OPP = range(4)
 CHIP_STEP = (0, 1, 3, 2)
 
@@ -26,8 +27,8 @@
 
 
 def kernel(n, x, dy, gate, up, wg_in, wu_in, wd_in,
-           dx, dwg, dwu, dwd, dyf, xf, dgs, dus, sibr, sumr,
-           wd, wg, wu, accd, accg, accu, act, gb, ub, dgb, dub, hb, sibst, sumst, last,
+           last, wg, wu, sibst, accd, dyf, xf, dgs, dus, sibr, sumr,
+           wd, accg, accu, act, gb, ub, dgb, dub, hb, sumst,
            send, recv, lsem, ssem, wsem):
     rows, d = x.shape
     f = gate.shape[1]
@@ -306,11 +307,8 @@
 
     csib[LEFT].wait_send()
     csib[OPP].wait_send()
-    outs = []
     for i in range(f // rows):
         sibst[i] = accd[i * rows : (i + 1) * rows, :].astype(BF16)
-        outs.append(load(sibst.at[i], at(dwd, i * rows, rows), wsem.at[i]))
-        outs[-1].start()
 
     blocks(4, near_place, ready_near(cx), begin_x(None), from_x)
 
@@ -332,36 +330,31 @@
     cx[FWD_NEG].wait_recv()
     cx[SIB + OPP].start()
     blocks(2, far_place, ready_far(cx), begin_x(None), from_x)
-    for o in outs:
-        o.wait()
-
-    outs = []
+
     for i in range(d // rows):
-        b = i % 2
-        if i >= 2:
-            outs[2 * i - 4].wait()
-            outs[2 * i - 3].wait()
         r = slice(i * rows, (i + 1) * rows)
-        gb[b] = accg[r, :].astype(BF16)
-        outs.append(load(gb.at[b], at(dwg, i * rows, rows), lsem.at[b, 1]))
-        outs[-1].start()
-        ub[b] = accu[r, :].astype(BF16)
-        outs.append(load(ub.at[b], at(dwu, i * rows, rows), lsem.at[b, 2]))
-        outs[-1].start()
-    for o in outs[-4:]:
-        o.wait()
-
-    outs = []
-    for i in range(2):
-        c3[i].wait_recv()
-        r = slice(i * half, (i + 1) * half)
-        act[0, r, :] = (accd[r, :] + last[i].astype(F32)).astype(BF16)
-        outs.append(load(act.at[0, pl.ds(i * half, half)], at(dx, i * half, half), lsem.at[i, 0]))
-        outs[-1].start()
-    for o in outs:
-        o.wait()
+        wg[r, :] = accg[r, :].astype(BF16)
+        wu[r, :] = accu[r, :].astype(BF16)
+    for c in c3:
+        c.wait_recv()
     for c in (*cdy.values(), *cx.values(), *c1, *c3):
         c.wait_send()
+
+
+def finish(last, dwg_in, dwu_in, dwd_in, held, dx, dwg, dwu, dwd, dxb, sem):
+    half = last.shape[1]
+    rows = 2 * half
+    copies = [pltpu.make_async_copy(s, t, sem.at[i]) for i, (s, t) in enumerate(((dwg_in, dwg), (dwu_in, dwu)))]
+    copies += [pltpu.make_async_copy(dwd_in.at[i], dwd.at[pl.ds(i * rows, rows)], sem.at[2 + i]) for i in range(dwd_in.shape[0])]
+    for c in copies:
+        c.start()
+    for i in range(2):
+        r = slice(i * half, (i + 1) * half)
+        dxb[r, :] = (held[r, :] + last[i].astype(F32)).astype(BF16)
+    copies.append(pltpu.make_async_copy(dxb, dx, sem.at[len(copies)]))
+    copies[-1].start()
+    for c in copies:
+        c.wait()
 
 
 def solution(mesh):
@@ -371,7 +364,7 @@
         rows, d = x.shape
         tokens, f = gate.shape
         half = rows // 2
-        hbm = pl.BlockSpec(memory_space=pltpu.HBM)
+        hbm, vmem = pl.BlockSpec(memory_space=pltpu.HBM), pl.BlockSpec(memory_space=pltpu.VMEM)
         s = lambda *shape: jax.ShapeDtypeStruct(shape, BF16)
         v = lambda *shape: pltpu.VMEM(shape, BF16)
         a = lambda *shape: pltpu.VMEM(shape, F32)
@@ -379,20 +372,30 @@
         flops = 12 * tokens * d * f
         outs = pl.pallas_call(
             functools.partial(kernel, n),
-            out_shape=(s(rows, d), s(d, f), s(d, f), s(f, d), s(tokens, d), s(tokens, d), s(tokens, f), s(tokens, f), s(4 * rows, d), s(4 * half, d)),
+            out_shape=(
+                v(2, half, d), v(d, f), v(d, f), v(f // rows, rows, d), a(f, d),
+                s(tokens, d), s(tokens, d), s(tokens, f), s(tokens, f), s(4 * rows, d), s(4 * half, d),
+            ),
             in_specs=[hbm] * 7,
-            out_specs=[hbm] * 10,
+            out_specs=[vmem] * 5 + [hbm] * 6,
             scratch_shapes=[
-                v(f, d), v(d, f), v(d, f), a(f, d), a(d, f), a(d, f),
-                v(2, rows, d), v(2, rows, f), v(2, rows, f), v(rows, f), v(rows, f), v(rows, f),
-                v(2, rows, d), v(4, half, d), v(2, half, d),
+                v(f, d), a(d, f), a(d, f),
+                v(2, rows, d), v(2, rows, f), v(2, rows, f), v(rows, f), v(rows, f), v(rows, f), v(4, half, d),
                 dma((N_COPIES,)), dma((N_COPIES,)), dma((2, 3)), dma((2,)), dma((3,)),
             ],
-            compiler_params=pltpu.CompilerParams(collective_id=0, has_side_effects=True, vmem_limit_bytes=67043328),
+            compiler_params=pltpu.CompilerParams(collective_id=0, has_side_effects=True, vmem_limit_bytes=LIMIT),
             cost_estimate=pl.CostEstimate(flops=flops, bytes_accessed=200 * 2**20, transcendentals=tokens * f),
             name="mlp_backward",
         )(x, dy, gate, up, wg, wu, wd)
-        return outs[:4]
+        return pl.pallas_call(
+            finish,
+            out_shape=(s(rows, d), s(d, f), s(d, f), s(f, d)),
+            in_specs=[vmem] * 5,
+            out_specs=[hbm] * 4,
+            scratch_shapes=[v(rows, d), dma((3 + f // rows,))],
+            compiler_params=pltpu.CompilerParams(vmem_limit_bytes=4 * 2**20),
+            name="finish",
+        )(*outs[:5])
 
     rows, columns = P(("dp", "tp"), None), P("dp", "tp")
     return jax.shard_map(

time: 224 us -> 215 us (0.960)
  local copies, waits for them, and re-layouts: 12.7 us -> 0 us
  Pallas kernels: 210 us -> 214 us
    unnamed x10 -> x0, local copies, waits for them, and re-layouts: 12.7 us -> none
    pallas_call x1 -> x2, Pallas kernels: 210 us -> 214 us  [the longest x1 208 us: local(): pl.pallas_call(functools.partial(kernel, n), out_shape=(v(2, half, d), v(...]
where the time goes in v2:
time: 215 us; the launch traced here: 214 us
  Pallas kernels  214 us (100%)
    pallas_call x1, Pallas kernels, local(): pl.pallas_call(functools.partial(kernel, n), out_shape=(v(2, half, d), v(...  208 us
    pallas_call x1, Pallas kernels, local(): pl.pallas_call(finish, out_shape=(s(rows, d), s(d, f), s(d, f), s(f, d)),...  5.27 us

profile of v2, /device:TPU:112, one launch (start us, length us, event | category | flops | bytes accessed | tf_op | source)
XLA Modules:
  0.0 214.3 jit_solution(17458266340724683943)
XLA Ops:
  0.6 208.2 %mlp_backward.1 = (bf16[2,256,2048]{2,1,0:T(8,128)(2,1)S(1)}, bf16[2048,1024]{1,0:T(8,128)(2,1)S(1)}, bf16[2048,1024]{1,0:T(8,128)(2,1)S(1)}, bf16[2,512,2048]{2...) custom-call(bf16[512,2048]{1,0:T(8,128)(2,1)} %x.1, ...), custom_call_target="tpu_custom_call" | custom-call | flops 103079215104 | bytes 209715200 | tf_op jit(solution)/shard_map/mlp_backward/pallas_call | solution.py:373
  208.9 5.3 %finish.1 = (bf16[512,2048]{1,0:T(8,128)(2,1)}, bf16[2048,1024]{1,0:T(8,128)(2,1)}, bf16[2048,1024]{1,0:T(8,128)(2,1)}, bf16[1024,2048]{1,0:T(8,128)(2,1)}) custom-call(bf16[2,256,2048]{2,1,0:T(8,128)(2,1)S(1)} %get-tuple-element.9.last, bf16[2048,1024]{1,0:T(8,128)(2,1)S(1)} %get-tuple-element.10.dwg_in, bf16[2048,1024]{1,0:T(8,128)(2,1)S(1)} %get-tuple-element.11.dwu_in, ...), custom_call_target="tpu_custom_call" | custom-call | tf_op jit(solution)/shard_map/finish/pallas_call | solution.py:390

commit v3 on v2

--- a/solution.py
+++ b/solution.py
@@ -27,9 +27,9 @@
 
 
 def kernel(n, x, dy, gate, up, wg_in, wu_in, wd_in,
-           last, wg, wu, sibst, accd, dyf, xf, dgs, dus, sibr, sumr,
+           early, passed, wg, wu, sibst, accd, dyf, xf, dgs, dus, sibr, sumr,
            wd, accg, accu, act, gb, ub, dgb, dub, hb, sumst,
-           send, recv, lsem, ssem, wsem):
+           send, recv, lsem, asem, ssem, wsem):
     rows, d = x.shape
     f = gate.shape[1]
     half = rows // 2
@@ -78,11 +78,12 @@
 
     cdy = gather_copies(0, dy, dyf)
     cx = gather_copies(X0, x, xf)
-    csib = [remote(SUM_SIB + q, sibst.at[q % 2], at(sibr, q * rows, rows), sib) for q in range(4)]
+    stage = {OWN: 0, OPP: 1, RIGHT: 0, LEFT: 1}
+    csib = [remote(SUM_SIB + q, sibst.at[stage[q]], at(sibr, q * rows, rows), sib) for q in range(4)]
     su = lambda i, s, to, dst: remote(i, sumst.at[s], dst, to)
     c2 = [su(U2_POS, 0, right, at(sumr, 0, half)), su(U2_NEG, 1, left, at(sumr, half, half))]
     c1 = [su(U1_POS, 2, right, at(sumr, 2 * half, half)), su(U1_NEG, 3, left, at(sumr, 3 * half, half))]
-    c3 = [su(U3_POS, 0, right, last.at[0]), su(U3_NEG, 1, left, last.at[1])]
+    c3 = [remote(i, passed.at[h], early.at[h], to) for i, h, to in ((U3_POS, 0, right), (U3_NEG, 1, left))]
 
     barrier = pltpu.get_barrier_semaphore()
     for other in (left, right, sib):
@@ -184,41 +185,62 @@
 
         lax.fori_loop(0, d // tile_d, columns, 0)
 
-    def dx_rows(r, count, adds, store):
-        loads = [load(at(dgs, r, count), gb.at[0, pl.ds(0, count)], lsem.at[0, 1]), load(at(dus, r, count), ub.at[0, pl.ds(0, count)], lsem.at[0, 2])]
-        bufs = [act.at[i, pl.ds(0, count)] for i in range(len(adds))]
-        loads += [load(a, t, lsem.at[i, 0]) for i, (a, t) in enumerate(zip(adds, bufs))]
-        for o in loads:
-            o.start()
-        for o in loads:
-            o.wait()
-
-        def columns(j, _):
-            c = pl.ds(pl.multiple_of(j * tile_d, tile_d), tile_d)
-            t = dot(gb[0, :count], wg[c, :], NT) + dot(ub[0, :count], wu[c, :], NT)
-            for o in bufs:
-                t += o[:, c].astype(F32)
-            store(c, t)
-            return 0
-
-        lax.fori_loop(0, d // tile_d, columns, 0)
-
-    def dx_for_sibling(q):
-        if q >= 2:
-            csib[q - 2].wait_send()
-
+    def dx_jobs(*jobs):
+        def loads(k):
+            r, count, adds, *_ = jobs[k]
+            b = k % 2
+            copies = []
+            if r is not None:
+                copies.append(load(at(dgs, r, count), gb.at[b, pl.ds(0, count)], lsem.at[b, 1]))
+                copies.append(load(at(dus, r, count), ub.at[b, pl.ds(0, count)], lsem.at[b, 2]))
+            for i, a in enumerate(adds):
+                copies.append(load(a, act.at[b, pl.ds(i * half, half)], asem.at[b, i]))
+            return copies
+
+        def begin(k):
+            for c in jobs[k][3]:
+                c.wait_recv()
+            for c in loads(k):
+                c.start()
+
+        begin(0)
+        for k, (r, count, adds, _, store, after) in enumerate(jobs):
+            if k + 1 < len(jobs):
+                begin(k + 1)
+            for c in loads(k):
+                c.wait()
+            b = k % 2
+            g, u = (gb.at[b], ub.at[b]) if r is not None else (dgb, dub)
+
+            def columns(j, _, g=g, u=u, b=b, count=count, adds=adds, store=store):
+                c = pl.ds(pl.multiple_of(j * tile_d, tile_d), tile_d)
+                t = dot(g[:count, :], wg[c, :], NT) + dot(u[:count, :], wu[c, :], NT)
+                for i in range(len(adds)):
+                    t += act[b, i * half : (i + 1) * half, c].astype(F32)
+                store(c, t)
+                return 0
+
+            lax.fori_loop(0, d // tile_d, columns, 0)
+            after()
+
+    def put(into):
         def store(c, t):
-            sibst[q % 2, :, c] = t.astype(BF16)
-
-        dx_rows(slot(q, 1), rows, [], store)
-        csib[q].start()
-
-    def dx_sum(q, h, s, extra, copy):
-        def store(c, t):
-            sumst[s, :, c] = t.astype(BF16)
-
-        dx_rows(slot(q, 0, h), half, [at(sibr, q * rows + h * half, half), *extra], store)
-        copy.start()
+            into[:, c] = t.astype(BF16)
+
+        return store
+
+    def for_sibling(q, here=False, before=None, after=None):
+        def done():
+            csib[q].start()
+            if before is not None:
+                before.wait_send()
+            if after is not None:
+                after()
+
+        return (None if here else slot(q, 1), rows, [], [], put(sibst.at[stage[q]]), done)
+
+    def chip_sum(q, h, into, extra, ready, after):
+        return (slot(q, 0, h), half, [at(sibr, q * rows + h * half, half), *extra], ready, put(into), after)
 
     def zero(ref):
         def body(i, _):
@@ -245,7 +267,7 @@
     blocks(2, own_place, ready_own(cdy), begin_dy(dy), from_dy)
     weights[1].wait()
     weights[2].wait()
-    dx_for_sibling(OWN)
+    dx_jobs(for_sibling(OWN, here=True))
 
     cdy[POS_A].wait_recv()
     cdy[NEG_B].wait_recv()
@@ -275,12 +297,6 @@
     cdy[FWD_POS].wait_recv()
     cdy[FWD_NEG].wait_recv()
     cdy[SIB + OPP].start()
-    dx_for_sibling(RIGHT)
-    dx_for_sibling(LEFT)
-    csib[RIGHT].wait_recv()
-    dx_sum(RIGHT, 1, 0, [], c2[0])
-    csib[LEFT].wait_recv()
-    dx_sum(LEFT, 0, 1, [], c2[1])
 
     def ready_far(copies):
         def ready(i):
@@ -291,68 +307,150 @@
 
     far_place = lambda i: (OPP, i)
     blocks(2, far_place, ready_far(cdy), begin_dy(None), from_dy)
-    dx_for_sibling(OPP)
-    csib[OPP].wait_recv()
-    dx_sum(OPP, 0, 2, [], c1[0])
-    dx_sum(OPP, 1, 3, [], c1[1])
-
-    cx[POS_A].wait_recv()
-    cx[NEG_B].wait_recv()
-    cx[FWD_POS].start()
-    cx[FWD_NEG].start()
+
+    def forward_x():
+        cx[POS_A].wait_recv()
+        cx[NEG_B].wait_recv()
+        cx[FWD_POS].start()
+        cx[FWD_NEG].start()
+
+    dx_jobs(
+        for_sibling(OPP, here=True, before=csib[OWN]),
+        for_sibling(RIGHT, before=csib[OPP], after=forward_x),
+        for_sibling(LEFT),
+        chip_sum(OPP, 0, sumst.at[2], [], [csib[OPP]], c1[0].start),
+        chip_sum(OPP, 1, sumst.at[3], [], [], c1[1].start),
+        chip_sum(RIGHT, 1, sumst.at[0], [], [csib[RIGHT]], c2[0].start),
+        chip_sum(LEFT, 0, sumst.at[1], [], [csib[LEFT]], c2[1].start),
+    )
+
     cx[POS_B].wait_recv()
     cx[NEG_A].wait_recv()
     cx[SIB + RIGHT].start()
     cx[SIB + LEFT].start()
 
+    csib[RIGHT].wait_send()
     csib[LEFT].wait_send()
-    csib[OPP].wait_send()
     for i in range(f // rows):
         sibst[i] = accd[i * rows : (i + 1) * rows, :].astype(BF16)
 
     blocks(4, near_place, ready_near(cx), begin_x(None), from_x)
 
-    csib[OWN].wait_recv()
-    for h, i in ((1, 0), (0, 1)):
-        c2[i].wait_recv()
-
-        def store(c, t, h=h):
+
+    def hold(h):
+        def store(c, t):
             accd[h * half : (h + 1) * half, c] = t
 
-        dx_rows(slot(OWN, 0, h), half, [at(sibr, h * half, half), at(sumr, i * half, half)], store)
-
-    for q, h, i in ((RIGHT, 0, 0), (LEFT, 1, 1)):
-        c1[i].wait_recv()
-        c2[i].wait_send()
-        dx_sum(q, h, i, [at(sumr, (2 + i) * half, half)], c3[i])
+        ready = [csib[OWN]] if h == 0 else []
+        return (slot(OWN, 0, h), half, [at(sibr, h * half, half)], ready, store, lambda: None)
+
+    dx_jobs(hold(0), hold(1))
 
     cx[FWD_POS].wait_recv()
     cx[FWD_NEG].wait_recv()
     cx[SIB + OPP].start()
     blocks(2, far_place, ready_far(cx), begin_x(None), from_x)
 
+    def passing(i, q, h):
+        def after():
+            @pl.when(core == 1)
+            def _():
+                c3[i].start()
+
+        return chip_sum(q, h, passed.at[i], [at(sumr, (2 + i) * half, half)], [c1[i]], after)
+
+    dx_jobs(passing(0, RIGHT, 0), passing(1, LEFT, 1))
+
     for i in range(d // rows):
         r = slice(i * rows, (i + 1) * rows)
         wg[r, :] = accg[r, :].astype(BF16)
         wu[r, :] = accu[r, :].astype(BF16)
-    for c in c3:
+    for c in c2:
         c.wait_recv()
-    for c in (*cdy.values(), *cx.values(), *c1, *c3):
+    for c in (*cdy.values(), *cx.values(), *c1, *c2):
         c.wait_send()
 
-
-def finish(last, dwg_in, dwu_in, dwd_in, held, dx, dwg, dwu, dwd, dxb, sem):
-    half = last.shape[1]
+    @pl.when(core == 1)
+    def _():
+        for c in c3:
+            c.wait_recv()
+            c.wait_send()
+
+
+def write_weights(dwg_in, dwu_in, dwd_in, own, sumr, early, held, dwg, dwu, dwd, token, near, sem):
+    core = lax.rem(lax.axis_index("tp"), 2)
+    half = near.shape[1]
     rows = 2 * half
-    copies = [pltpu.make_async_copy(s, t, sem.at[i]) for i, (s, t) in enumerate(((dwg_in, dwg), (dwu_in, dwu)))]
-    copies += [pltpu.make_async_copy(dwd_in.at[i], dwd.at[pl.ds(i * rows, rows)], sem.at[2 + i]) for i in range(dwd_in.shape[0])]
+    adds = [pltpu.make_async_copy(sumr.at[pl.ds((1 - h) * half, half)], near.at[h], sem.at[h]) for h in range(2)]
+    more = [pltpu.make_async_copy(early.at[h], near.at[2 + h], sem.at[2 + h]) for h in range(2)]
+    copies = [pltpu.make_async_copy(s, t, sem.at[4 + i]) for i, (s, t) in enumerate(((dwg_in, dwg), (dwu_in, dwu)))]
+    copies += [pltpu.make_async_copy(dwd_in.at[i], dwd.at[pl.ds(i * rows, rows)], sem.at[6 + i]) for i in range(dwd_in.shape[0])]
+    for c in (*adds, *copies):
+        c.start()
+    token[...] = jnp.zeros_like(token)
+
+    @pl.when(core == 1)
+    def _():
+        for c in more:
+            c.start()
+
+    for h in range(2):
+        adds[h].wait()
+        r = slice(h * half, (h + 1) * half)
+        held[r, :] = own[r, :] + near[h].astype(F32)
+
+    @pl.when(core == 1)
+    def _():
+        for h in range(2):
+            more[h].wait()
+            r = slice(h * half, (h + 1) * half)
+            held[r, :] += near[2 + h].astype(F32)
+
     for c in copies:
-        c.start()
-    for i in range(2):
-        r = slice(i * half, (i + 1) * half)
-        dxb[r, :] = (held[r, :] + last[i].astype(F32)).astype(BF16)
-    copies.append(pltpu.make_async_copy(dxb, dx, sem.at[len(copies)]))
-    copies[-1].start()
+        c.wait()
+
+
+def pass_on(n, passed, token, late, send, recv):
+    me = lax.axis_index("tp")
+    core = lax.rem(me, 2)
+    right, left = lax.rem(me + 2, n), lax.rem(me + n - 2, n)
+    half = passed.shape[1]
+    barrier = pltpu.get_barrier_semaphore()
+    for other in (left, right):
+        pl.semaphore_signal(barrier, inc=1, device_id={"tp": other}, device_id_type=MESH)
+    pl.semaphore_wait(barrier, 2)
+
+    @pl.when(core == 0)
+    def _():
+        copies = [
+            pltpu.make_async_remote_copy(
+                src_ref=passed.at[h], dst_ref=late.at[h], send_sem=send.at[h], recv_sem=recv.at[h],
+                device_id={"tp": to}, device_id_type=MESH)
+            for h, to in enumerate((right, left))
+        ]
+        for c in copies:
+            c.start()
+        for c in copies:
+            c.wait()
+
+
+def finish(held, late, dx, dxb, sem):
+    core = lax.rem(lax.axis_index("tp"), 2)
+    half = late.shape[1]
+    copies = []
+    for h in range(2):
+        r = pl.ds(h * half, half)
+
+        @pl.when(core == 0)
+        def _(r=r, h=h):
+            dxb[r, :] = (held[r, :] + late[h].astype(F32)).astype(BF16)
+
+        @pl.when(core == 1)
+        def _(r=r):
+            dxb[r, :] = held[r, :].astype(BF16)
+
+        copies.append(pltpu.make_async_copy(dxb.at[r], dx.at[r], sem.at[h]))
+        copies[-1].start()
     for c in copies:
         c.wait()
 
@@ -370,32 +468,53 @@
         a = lambda *shape: pltpu.VMEM(shape, F32)
         dma = pltpu.SemaphoreType.DMA
         flops = 12 * tokens * d * f
-        outs = pl.pallas_call(
+        early, passed, dwg, dwu, dwd, own, *_, sumr = pl.pallas_call(
             functools.partial(kernel, n),
             out_shape=(
-                v(2, half, d), v(d, f), v(d, f), v(f // rows, rows, d), a(f, d),
-                s(tokens, d), s(tokens, d), s(tokens, f), s(tokens, f), s(4 * rows, d), s(4 * half, d),
+                pltpu.HBM((2, half, d), BF16), v(2, half, d), v(d, f), v(d, f), v(f // rows, rows, d), a(f, d),
+                s(tokens, d), s(tokens, d), s(tokens, f), s(tokens, f), s(4 * rows, d), pltpu.HBM((4 * half, d), BF16),
             ),
             in_specs=[hbm] * 7,
-            out_specs=[vmem] * 5 + [hbm] * 6,
+            out_specs=[hbm] + [vmem] * 5 + [hbm] * 6,
             scratch_shapes=[
                 v(f, d), a(d, f), a(d, f),
                 v(2, rows, d), v(2, rows, f), v(2, rows, f), v(rows, f), v(rows, f), v(rows, f), v(4, half, d),
-                dma((N_COPIES,)), dma((N_COPIES,)), dma((2, 3)), dma((2,)), dma((3,)),
+                dma((N_COPIES,)), dma((N_COPIES,)), dma((2, 3)), dma((2, 2)), dma((2,)), dma((3,)),
             ],
             compiler_params=pltpu.CompilerParams(collective_id=0, has_side_effects=True, vmem_limit_bytes=LIMIT),
             cost_estimate=pl.CostEstimate(flops=flops, bytes_accessed=200 * 2**20, transcendentals=tokens * f),
             name="mlp_backward",
         )(x, dy, gate, up, wg, wu, wd)
-        return pl.pallas_call(
+        in_vmem = lambda t: pltpu.with_memory_space_constraint(t, pltpu.VMEM)
+        small = pltpu.CompilerParams(vmem_limit_bytes=8 * 2**20)
+        held, dwg, dwu, dwd, token = pl.pallas_call(
+            write_weights,
+            out_shape=(a(rows, d), s(d, f), s(d, f), s(f, d), v(8, 128)),
+            in_specs=[vmem] * 4 + [hbm] * 2,
+            out_specs=[vmem, hbm, hbm, hbm, vmem],
+            scratch_shapes=[v(4, half, d), dma((6 + f // rows,))],
+            compiler_params=small,
+            name="write_weights",
+        )(*map(in_vmem, (dwg, dwu, dwd, own)), *(pltpu.with_memory_space_constraint(t, pltpu.HBM) for t in (sumr, early)))
+        late = pl.pallas_call(
+            functools.partial(pass_on, n),
+            out_shape=v(2, half, d),
+            in_specs=[vmem] * 2,
+            out_specs=vmem,
+            scratch_shapes=[dma((2,)), dma((2,))],
+            compiler_params=pltpu.CompilerParams(collective_id=1, has_side_effects=True, vmem_limit_bytes=8 * 2**20),
+            name="pass_on",
+        )(in_vmem(passed), in_vmem(token))
+        dx = pl.pallas_call(
             finish,
-            out_shape=(s(rows, d), s(d, f), s(d, f), s(f, d)),
-            in_specs=[vmem] * 5,
-            out_specs=[hbm] * 4,
-            scratch_shapes=[v(rows, d), dma((3 + f // rows,))],
-            compiler_params=pltpu.CompilerParams(vmem_limit_bytes=4 * 2**20),
+            out_shape=s(rows, d),
+            in_specs=[vmem] * 2,
+            out_specs=hbm,
+            scratch_shapes=[v(rows, d), dma((2,))],
+            compiler_params=small,
             name="finish",
-        )(*outs[:5])
+        )(*map(in_vmem, (held, late)))
+        return dx, dwg, dwu, dwd
 
     rows, columns = P(("dp", "tp"), None), P("dp", "tp")
     return jax.shard_map(

time: 215 us -> 210 us (0.977)
  Pallas kernels: 214 us -> 209 us
    pallas_call x2 -> x4, Pallas kernels: 214 us -> 209 us  [the longest x1 187 us: local(): pl.pallas_call(functools.partial(kernel, n), out_shape=(pltpu.HBM((2, hal...]
where the time goes in v3:
time: 210 us
  Pallas kernels  209 us (100%)
    pallas_call x1, Pallas kernels, local(): pl.pallas_call(functools.partial(kernel, n), out_shape=(pltpu.HBM((2, hal...  187 us
    pallas_call x1, Pallas kernels, local(): pl.pallas_call(functools.partial(pass_on, n), out_shape=v(2, half, d), in...  16.2 us
    pallas_call x1, Pallas kernels, local(): pl.pallas_call(write_weights, out_shape=(a(rows, d), s(d, f), s(d, f), s(...  4.75 us

profile of v3, /device:TPU:112, one launch (start us, length us, event | category | flops | bytes accessed | tf_op | source)
XLA Modules:
  0.0 209.9 jit_solution(16487451756209287369)
XLA Ops:
  0.6 186.6 %mlp_backward.1 = (bf16[2,256,2048]{2,1,0:T(8,128)(2,1)}, bf16[2,256,2048]{2,1,0:T(8,128)(2,1)S(1)}, bf16[2048,1024]{1,0:T(8,128)(2,1)S(1)}, bf16[2048,1024]{1,0...) custom-call(bf16[512,2048]{1,0:T(8,128)(2,1)} %x.1, ...), custom_call_target="tpu_custom_call" | custom-call | flops 103079215104 | bytes 209715200 | tf_op jit(solution)/shard_map/mlp_backward/pallas_call | solution.py:471
  187.3 4.7 %write_weights.1 = (f32[512,2048]{1,0:T(8,128)S(1)}, bf16[2048,1024]{1,0:T(8,128)(2,1)}, bf16[2048,1024]{1,0:T(8,128)(2,1)}, bf16[1024,2048]{1,0:T(8,128)(2,1)}, bf16[8,128]{1,0:T(8,128)(2,1)S(1)}) custom-call(bf16[2048,1024]{1,0:T(8,128)(2,1)S(1)} %get-tuple-element.16.dwg_in, bf16[2048,1024]{1,0:T(8,128)(2,1)S(1)} %get-tuple-element.17.dwu_in, ...), custom_call_target="tpu_custom_call" | custom-call | tf_op jit(solution)/shard_map/write_weights/pallas_call | solution.py:490
  192.0 16.2 %pass_on.1.late = bf16[2,256,2048]{2,1,0:T(8,128)(2,1)S(1)} custom-call(bf16[2,256,2048]{2,1,0:T(8,128)(2,1)S(1)} %get-tuple-element.23.passed, bf16[8,128]{1,0:T(8,128)(2,1)S(1)} %get-tuple-element.24.token), custom_call_target="tpu_custom_call" | custom-call | tf_op jit(solution)/shard_map/pass_on/pallas_call | solution.py:499
  208.2 1.5 finish.1

commit v4 on v3

--- a/solution.py
+++ b/solution.py
@@ -12,6 +12,7 @@
 TN = (((0,), (0,)), ((), ()))
 F32, BF16 = jnp.float32, jnp.bfloat16
 LIMIT = 41 * 2**20
+LATE = 0
 OWN, RIGHT, LEFT, OPP = range(4)
 CHIP_STEP = (0, 1, 3, 2)
 
@@ -353,7 +354,7 @@
 
     def passing(i, q, h):
         def after():
-            @pl.when(core == 1)
+            @pl.when(core != LATE)
             def _():
                 c3[i].start()
 
@@ -370,7 +371,7 @@
     for c in (*cdy.values(), *cx.values(), *c1, *c2):
         c.wait_send()
 
-    @pl.when(core == 1)
+    @pl.when(core != LATE)
     def _():
         for c in c3:
             c.wait_recv()
@@ -389,7 +390,7 @@
         c.start()
     token[...] = jnp.zeros_like(token)
 
-    @pl.when(core == 1)
+    @pl.when(core != LATE)
     def _():
         for c in more:
             c.start()
@@ -399,7 +400,7 @@
         r = slice(h * half, (h + 1) * half)
         held[r, :] = own[r, :] + near[h].astype(F32)
 
-    @pl.when(core == 1)
+    @pl.when(core != LATE)
     def _():
         for h in range(2):
             more[h].wait()
@@ -410,7 +411,7 @@
         c.wait()
 
 
-def pass_on(n, passed, token, late, send, recv):
+def pass_on(n, passed, held, token, dx, late, send, recv):
     me = lax.axis_index("tp")
     core = lax.rem(me, 2)
     right, left = lax.rem(me + 2, n), lax.rem(me + n - 2, n)
@@ -420,37 +421,35 @@
         pl.semaphore_signal(barrier, inc=1, device_id={"tp": other}, device_id_type=MESH)
     pl.semaphore_wait(barrier, 2)
 
-    @pl.when(core == 0)
+    @pl.when(core == LATE)
     def _():
-        copies = [
-            pltpu.make_async_remote_copy(
-                src_ref=passed.at[h], dst_ref=late.at[h], send_sem=send.at[h], recv_sem=recv.at[h],
-                device_id={"tp": to}, device_id_type=MESH)
-            for h, to in enumerate((right, left))
-        ]
-        for c in copies:
-            c.start()
-        for c in copies:
-            c.wait()
-
-
-def finish(held, late, dx, dxb, sem):
-    core = lax.rem(lax.axis_index("tp"), 2)
-    half = late.shape[1]
-    copies = []
-    for h in range(2):
-        r = pl.ds(h * half, half)
-
-        @pl.when(core == 0)
-        def _(r=r, h=h):
-            dxb[r, :] = (held[r, :] + late[h].astype(F32)).astype(BF16)
-
-        @pl.when(core == 1)
-        def _(r=r):
-            dxb[r, :] = held[r, :].astype(BF16)
-
-        copies.append(pltpu.make_async_copy(dxb.at[r], dx.at[r], sem.at[h]))
-        copies[-1].start()
+        copies = []
+        for k, (start, count) in enumerate(((0, half - half // 8), (half - half // 8, half // 8))):
+            for h, to in enumerate((right, left)):
+                r = pl.ds(start, count)
+                c = pltpu.make_async_remote_copy(
+                    src_ref=passed.at[h, r], dst_ref=late.at[h, r], send_sem=send.at[h, k], recv_sem=recv.at[h, k],
+                    device_id={"tp": to}, device_id_type=MESH)
+                c.start()
+                copies.append((c, h, start, count))
+        for c, h, start, count in copies:
+            c.wait_recv()
+            r = slice(h * half + start, h * half + start + count)
+            dx[r, :] = (held[r, :] + late[h, start : start + count, :].astype(F32)).astype(BF16)
+        for c, *_ in copies:
+            c.wait_send()
+
+    @pl.when(core != LATE)
+    def _():
+        dx[...] = held[...].astype(BF16)
+
+
+def finish(dx_in, dx, sem):
+    parts = sem.shape[0]
+    count = dx.shape[0] // parts
+    copies = [pltpu.make_async_copy(dx_in.at[r], dx.at[r], sem.at[i]) for i in range(parts) for r in (pl.ds(i * count, count),)]
+    for c in copies:
+        c.start()
     for c in copies:
         c.wait()
 
@@ -496,24 +495,24 @@
             compiler_params=small,
             name="write_weights",
         )(*map(in_vmem, (dwg, dwu, dwd, own)), *(pltpu.with_memory_space_constraint(t, pltpu.HBM) for t in (sumr, early)))
-        late = pl.pallas_call(
+        dx = pl.pallas_call(
             functools.partial(pass_on, n),
-            out_shape=v(2, half, d),
-            in_specs=[vmem] * 2,
+            out_shape=v(rows, d),
+            in_specs=[vmem] * 3,
             out_specs=vmem,
-            scratch_shapes=[dma((2,)), dma((2,))],
+            scratch_shapes=[v(2, half, d), dma((2, 2)), dma((2, 2))],
             compiler_params=pltpu.CompilerParams(collective_id=1, has_side_effects=True, vmem_limit_bytes=8 * 2**20),
             name="pass_on",
-        )(in_vmem(passed), in_vmem(token))
+        )(*map(in_vmem, (passed, held, token)))
         dx = pl.pallas_call(
             finish,
             out_shape=s(rows, d),
-            in_specs=[vmem] * 2,
+            in_specs=[vmem],
             out_specs=hbm,
-            scratch_shapes=[v(rows, d), dma((2,))],
+            scratch_shapes=[dma((1,))],
             compiler_params=small,
             name="finish",
-        )(*map(in_vmem, (held, late)))
+        )(in_vmem(dx))
         return dx, dwg, dwu, dwd
 
     rows, columns = P(("dp", "tp"), None), P("dp", "tp")

time: 210 us -> 210 us (level)
  no operation moved by 1% of the time
where the time goes in v4:
time: 210 us
  Pallas kernels  209 us (100%)
    pallas_call x1, Pallas kernels, local(): pl.pallas_call(functools.partial(kernel, n), out_shape=(pltpu.HBM((2, hal...  187 us
    pallas_call x1, Pallas kernels, local(): pl.pallas_call(functools.partial(pass_on, n), out_shape=v(rows, d), in_sp...  16.3 us
    pallas_call x1, Pallas kernels, local(): pl.pallas_call(write_weights, out_shape=(a(rows, d), s(d, f), s(d, f), s(...  4.75 us

profile of v4, /device:TPU:112, one launch (start us, length us, event | category | flops | bytes accessed | tf_op | source)
XLA Modules:
  0.0 209.8 jit_solution(8358692530761713128)
XLA Ops:
  0.6 186.6 %mlp_backward.1 = (bf16[2,256,2048]{2,1,0:T(8,128)(2,1)}, bf16[2,256,2048]{2,1,0:T(8,128)(2,1)S(1)}, bf16[2048,1024]{1,0:T(8,128)(2,1)S(1)}, bf16[2048,1024]{1,0...) custom-call(bf16[512,2048]{1,0:T(8,128)(2,1)} %x.1, ...), custom_call_target="tpu_custom_call" | custom-call | flops 103079215104 | bytes 209715200 | tf_op jit(solution)/shard_map/mlp_backward/pallas_call | solution.py:470
  187.3 4.7 %write_weights.1 = (f32[512,2048]{1,0:T(8,128)S(1)}, bf16[2048,1024]{1,0:T(8,128)(2,1)}, bf16[2048,1024]{1,0:T(8,128)(2,1)}, bf16[1024,2048]{1,0:T(8,128)(2,1)}, bf16[8,128]{1,0:T(8,128)(2,1)S(1)}) custom-call(bf16[2048,1024]{1,0:T(8,128)(2,1)S(1)} %get-tuple-element.17.dwg_in, bf16[2048,1024]{1,0:T(8,128)(2,1)S(1)} %get-tuple-element.18.dwu_in, ...), custom_call_target="tpu_custom_call" | custom-call | tf_op jit(solution)/shard_map/write_weights/pallas_call | solution.py:489
  192.0 16.3 %pass_on.1.dx_in = bf16[512,2048]{1,0:T(8,128)(2,1)S(1)} custom-call(bf16[2,256,2048]{2,1,0:T(8,128)(2,1)S(1)} %get-tuple-element.16.passed, f32[512,2048]{1,0:T(8,128)S(1)} %get-tuple-element.23.held, bf16[8,128]{1,0:T(8,128)(2,1)S(1)} %get-tuple-element.24.token), custom_call_target="tpu_custom_call" | custom-call | tf_op jit(solution)/shard_map/pass_on/pallas_call | solution.py:498
  208.3 1.3 finish.1

commit v5 on v4

--- a/solution.py
+++ b/solution.py
@@ -424,7 +424,7 @@
     @pl.when(core == LATE)
     def _():
         copies = []
-        for k, (start, count) in enumerate(((0, half - half // 8), (half - half // 8, half // 8))):
+        for k, (start, count) in enumerate(((0, half - half // 16), (half - half // 16, half // 16))):
             for h, to in enumerate((right, left)):
                 r = pl.ds(start, count)
                 c = pltpu.make_async_remote_copy(

time: 210 us -> 210 us (level)
  no operation moved by 1% of the time
where the time goes in v5:
time: 210 us
  Pallas kernels  209 us (100%)
    pallas_call x1, Pallas kernels, local(): pl.pallas_call(functools.partial(kernel, n), out_shape=(pltpu.HBM((2, hal...  187 us
    pallas_call x1, Pallas kernels, local(): pl.pallas_call(functools.partial(pass_on, n), out_shape=v(rows, d), in_sp...  16.3 us
    pallas_call x1, Pallas kernels, local(): pl.pallas_call(write_weights, out_shape=(a(rows, d), s(d, f), s(d, f), s(...  4.75 us

profile of v5, /device:TPU:112, one launch (start us, length us, event | category | flops | bytes accessed | tf_op | source)
XLA Modules:
  0.0 209.8 jit_solution(4924470258455166981)
XLA Ops:
  0.6 186.6 %mlp_backward.1 = (bf16[2,256,2048]{2,1,0:T(8,128)(2,1)}, bf16[2,256,2048]{2,1,0:T(8,128)(2,1)S(1)}, bf16[2048,1024]{1,0:T(8,128)(2,1)S(1)}, bf16[2048,1024]{1,0...) custom-call(bf16[512,2048]{1,0:T(8,128)(2,1)} %x.1, ...), custom_call_target="tpu_custom_call" | custom-call | flops 103079215104 | bytes 209715200 | tf_op jit(solution)/shard_map/mlp_backward/pallas_call | solution.py:470
  187.3 4.7 %write_weights.1 = (f32[512,2048]{1,0:T(8,128)S(1)}, bf16[2048,1024]{1,0:T(8,128)(2,1)}, bf16[2048,1024]{1,0:T(8,128)(2,1)}, bf16[1024,2048]{1,0:T(8,128)(2,1)}, bf16[8,128]{1,0:T(8,128)(2,1)S(1)}) custom-call(bf16[2048,1024]{1,0:T(8,128)(2,1)S(1)} %get-tuple-element.17.dwg_in, bf16[2048,1024]{1,0:T(8,128)(2,1)S(1)} %get-tuple-element.18.dwu_in, ...), custom_call_target="tpu_custom_call" | custom-call | tf_op jit(solution)/shard_map/write_weights/pallas_call | solution.py:489
  192.0 16.3 %pass_on.1.dx_in = bf16[512,2048]{1,0:T(8,128)(2,1)S(1)} custom-call(bf16[2,256,2048]{2,1,0:T(8,128)(2,1)S(1)} %get-tuple-element.16.passed, f32[512,2048]{1,0:T(8,128)S(1)} %get-tuple-element.23.held, bf16[8,128]{1,0:T(8,128)(2,1)S(1)} %get-tuple-element.24.token), custom_call_target="tpu_custom_call" | custom-call | tf_op jit(solution)/shard_map/pass_on/pallas_call | solution.py:498
  208.3 1.3 finish.1
